TPU v7x, 32 devices: a whole 2x2x4 slice. The times are simulated.
32 devices in a mesh: gx: 4 (over z), gy: 8 (over y, x, core).
Axes of the slice: x: 2, y: 2, z: 4, core: 2. Of those that a mesh axis runs over, the one named last changes fastest.
Arguments:
- prolong: bfloat16 [2048, 24, 128], P(('gx', 'gy')), may hold values from -0.5 to 0.5
- stiffness: bfloat16 [4096, 4, 128, 128], P(('gx', 'gy')), may hold values from -6 to 6
- request: int32 [4096], P(('gx', 'gy')), may hold values from 0 to 63, as said below
- col_slot: int32 [4096, 4], P(('gx', 'gy')), may hold values from 0 to 127
- col_pos: int32 [4096, 4], P(('gx', 'gy')), may hold values from 0 to 15, as said below
- coarse_owner: int32 [2048, 1], P(('gx', 'gy')), may hold values from 0 to 31; in each aligned block of 64 rows (0 to 63, 64 to 127, ...) at most 4 rows name the same one
Outputs:
- coarse: float32 [4096, 24, 384], P(('gx', 'gy'))
Inputs may be any that keep to these rules, and one draw needn't show every extreme that they name: `request`: on each device, entries k * 4 to (k + 1) * 4 - 1 name distinct aggregates of device k, as local indices there. `col_pos`: the 4 entries of one block row are distinct. `coarse_owner`: among one device's 64 aggregates at most 4 share a coarse owner, and on some devices 4 do.
All inputs are finite; a program needn't handle non-finite values.
Results may differ from a plain program's by a relative error of at most 0.0003.
Values may be sent and summed in bfloat16 or wider, within the bound.
A program may use at most 128 MiB of HBM per device.

v0:
```python
import jax
import jax.numpy as jnp
from jax import lax
from jax.sharding import PartitionSpec as P

MAXNB = 16


HIGH = lax.Precision.HIGHEST


def placed(partial_value, column_hot):
    spread = jnp.einsum("tqce,tqn->tcne", partial_value, column_hot, precision=HIGH)
    return spread.reshape(
        partial_value.shape[0], partial_value.shape[2], column_hot.shape[2] * partial_value.shape[3]
    )


def per_device(prolong, stiffness, request, col_slot, col_pos, coarse_owner):
    devices = lax.axis_size(("gx", "gy"))
    own_aggs = prolong.shape[0]
    columns = MAXNB
    requested = lax.all_to_all(request, ("gx", "gy"), split_axis=0, concat_axis=0, tiled=True)
    fetched = lax.all_to_all(
        prolong[requested], ("gx", "gy"), split_axis=0, concat_axis=0, tiled=True
    )
    col_rows = fetched[col_slot]
    applied = jnp.einsum("tqij,tqej->tqei", stiffness, col_rows, preferred_element_type=jnp.float32)
    partial_value = jnp.einsum(
        "tci,tqei->tqce", fetched.astype(jnp.float32), applied, precision=HIGH
    )
    blocks_in, where_in = (
        lax.all_to_all(partial_value, ("gx", "gy"), split_axis=0, concat_axis=0, tiled=True),
        lax.all_to_all(
            col_pos.astype(jnp.float32), ("gx", "gy"), split_axis=0, concat_axis=0, tiled=True
        ),
    )
    hot_in = (where_in[:, :, None] == jnp.arange(columns, dtype=jnp.float32)[None, None, :]).astype(
        jnp.float32
    )
    rows_in = placed(blocks_in, hot_in)
    owner_hot = (requested[None, :] == jnp.arange(own_aggs, dtype=jnp.int32)[:, None]).astype(
        jnp.float32
    )
    fine_rows = jnp.einsum("at,tcw->acw", owner_hot, rows_in, precision=HIGH)
    owners = coarse_owner[:, 0]
    peer_ids = jnp.arange(devices, dtype=jnp.int32)
    owner_one = (owners[:, None] == peer_ids[None, :]).astype(jnp.int32)
    before = jnp.cumsum(owner_one, axis=0) - owner_one
    row_rank = jnp.sum(before * owner_one, axis=1)
    send_max = (2 * own_aggs + devices - 1) // devices
    place_hot = (owners[None, None, :] == peer_ids[:, None, None]) & (
        row_rank[None, None, :] == jnp.arange(send_max, dtype=jnp.int32)[None, :, None]
    )
    outgoing = jnp.einsum("esa,acw->escw", place_hot.astype(jnp.float32), fine_rows, precision=HIGH)
    arrived = lax.all_to_all(outgoing, ("gx", "gy"), split_axis=0, concat_axis=0, tiled=True)
    return arrived.reshape((devices * send_max,) + fine_rows.shape[1:])


def solution(mesh):
    placed = (
        P(("gx", "gy"), None, None),
        P(("gx", "gy"), None, None, None),
        P(("gx", "gy")),
        P(("gx", "gy"), None),
        P(("gx", "gy"), None),
        P(("gx", "gy"), None),
    )
    return jax.shard_map(
        per_device,
        mesh=mesh,
        in_specs=placed,
        out_specs=P(("gx", "gy"), None, None),
        check_vma=False,
    )
```

profile of v0, /device:TPU:15, one launch (start us, length us, event | category | flops | bytes accessed | tf_op | source)
XLA Modules:
  0.0 277.1 jit_solution(11292029791068838315)
XLA Ops:
  0.0 0.8 all_to_all.23
  0.8 9.9 %all_to_all.36 = s32[32,4,1]{1,2,0:T(1,128)S(1)} all-to-all(s32[32,4,1]{1,2,0:T(1,128)S(1)} %bitcast.55), channel_id=1, replica_groups=mesh['gx'=4,'gy'=8] {'gx','gy'}, dimensions={0} | all-to-all | bytes 1024 | tf_op jit(solution)/shard_map/all_to_all | solution.py:23
  10.9 1.6 gather_fusion
  12.5 5.9 %all-to-all-start.2 = ((bf16[128,24,128]{2,1,0:T(8,128)(2,1)}), bf16[128,24,128]{2,1,0:T(8,128)(2,1)S(1)}, u32[]{:S(2)}, u32[]{:S(2)}) async-start(bf16[128,24,128]{2,1,0:T(8,128)(2,1)} %gather_fusion), calls=%async_computation.2 | async-start | bytes 1572864 | tf_op jit(solution)/shard_map/all_to_all | solution.py:24
  18.4 0.7 convert_element_type.5
  19.0 0.1 all_to_all.25
  19.2 0.7 copy.13
  19.8 0.7 compare_select_fusion
  20.5 0.1 copy.16
  20.7 15.7 %all-to-all-done.2 = bf16[128,24,128]{2,1,0:T(8,128)(2,1)S(1)} async-done(((bf16[128,24,128]{2,1,0:T(8,128)(2,1)}), bf16[128,24,128]{2,1,0:T(8,128)(2,1)S(1)}, u32[]{:S(2)}, u32[]{:S(2)}) %all-to-all-start.2) | async-done | bytes 786464 | tf_op jit(solution)/shard_map/all_to_all | solution.py:24
  36.4 6.1 %all-to-all-start.1 = ((f32[32,4,4]{1,2,0:T(4,128)}), f32[32,4,4]{1,2,0:T(4,128)S(1)}, u32[]{:S(2)}, u32[]{:S(2)}) async-start(f32[32,4,4]{1,2,0:T(4,128)} %copy.13), calls=%async_computation.1 | async-start | bytes 131072 | tf_op jit(solution)/shard_map/all_to_all | solution.py:34
  42.5 3.2 %gather_fusion.1 = bf16[512,24,128]{2,1,0:T(8,128)(2,1)} fusion(bf16[128,24,128]{2,1,0:T(8,128)(2,1)S(1)} %all-to-all-done.2, s32[1024]{0:T(1024)S(1)} %pad_clamp_fusion), kind=kCustom, calls=%fused_computation.1 | custom fusion | bytes 6293504 | tf_op jit(solution)/shard_map/gather | solution.py:27
  45.7 12.8 %fusion.19 = f32[128,4,24,128]{3,2,1,0:T(8,128)S(1)} fusion(bf16[128,4,24,128]{3,2,1,0:T(8,128)(2,1)} %bitcast.50, bf16[128,4,128,128]{3,2,1,0:T(8,128)(2,1)} %param.7), kind=kOutput, calls=%fused_computation.29 | convolution fusion | flops 402653184 | bytes 26214400 | tf_op jit(solution)/shard_map/tqij,tqej->tqei/dot_general | solution.py:28
  58.5 4.8 %fusion.16 = f32[128,4,24,24]{3,2,1,0:T(8,128)} fusion(f32[128,4,24,128]{3,2,1,0:T(8,128)S(1)} %fusion.19, bf16[128,24,128]{2,1,0:T(8,128)(2,1)S(1)} %all-to-all-done.2), kind=kOutput, calls=%fused_computation.28 | convolution fusion | flops 452984832 | bytes 8257536 | tf_op jit(solution)/shard_map/tci,tqei->tqce/dot_general | solution.py:29
  63.3 7.2 %reshape.128 = f32[32,1,9216]{2,1,0:T(1,128)} reshape(f32[128,4,24,24]{3,2,1,0:T(8,128)} %fusion.16) | data formatting | bytes 2359296
  70.5 5.8 %all-to-all-start.3 = ((f32[32,1,9216]{2,1,0:T(1,128)}), f32[32,1,9216]{2,1,0:T(1,128)S(1)}, u32[]{:S(2)}, u32[]{:S(2)}) async-start(f32[32,1,9216]{2,1,0:T(1,128)} %reshape.128), calls=%async_computation.3 | async-start | bytes 2359296 | tf_op jit(solution)/shard_map/all_to_all | solution.py:33
  76.5 0.2 select_reduce_fusion
  76.8 0.6 broadcast.62
  77.3 0.7 reduce.5
  78.2 0.3 copy.25
  78.5 23.8 %all-to-all-done.3 = f32[32,1,9216]{2,1,0:T(1,128)S(1)} async-done(((f32[32,1,9216]{2,1,0:T(1,128)}), f32[32,1,9216]{2,1,0:T(1,128)S(1)}, u32[]{:S(2)}, u32[]{:S(2)}) %all-to-all-start.3) | async-done | bytes 1179680 | tf_op jit(solution)/shard_map/all_to_all | solution.py:33
  102.3 0.5 broadcast.63
  102.8 3.4 %reduce.6 = f32[32,9216]{1,0:T(8,128)S(1)} reduce(f32[32,1,9216]{2,1,0:T(1,128)S(1)} %all-to-all-done.3, f32[]{:T(128)} %broadcast.63), dimensions={1}, to_apply=%all_to_all.29.reduce_sub_computation | reduce | bytes 2359300 | tf_op jit(solution)/shard_map/all_to_all | solution.py:33
  106.2 6.3 %reshape.129 = f32[128,4,24,24]{3,2,1,0:T(8,128)} reshape(f32[32,9216]{1,0:T(8,128)S(1)} %reduce.6) | data formatting | bytes 2359296
  112.5 8.6 %copy.17 = f32[128,4,24,24]{3,1,2,0:T(4,128)} copy(f32[128,4,24,24]{2,3,1,0:T(8,128)} %bitcast.49) | data formatting | bytes 2359296 | tf_op jit(solution)/shard_map/all_to_all | solution.py:33
  121.1 19.0 %convolution_bitcast_fusion = f32[128,24,16,24]{3,2,1,0:T(8,128)} fusion(f32[128,4,24,24]{3,1,2,0:T(4,128)} %copy.17, f32[128,4]{1,0:T(8,128)S(1)} %bitcast.53), kind=kOutput, calls=%fused_computation.2 | convolution fusion | flops 56631296 | bytes 5900288 | tf_op jit(solution)/shard_map/tqce,tqn->tcne/dot_general | solution.py:13
  140.1 15.4 %copy.18 = f32[128,24,16,24]{0,3,2,1:T(8,128)} copy(f32[128,24,16,24]{3,2,1,0:T(8,128)} %convolution_bitcast_fusion) | data formatting | bytes 9437184 | tf_op jit(solution)/shard_map/tqce,tqn->tcne/transpose | solution.py:13
  155.6 5.2 %fusion.10 = f32[64,24,384]{2,0,1:T(8,128)S(1)} fusion(f32[128,24,384]{0,2,1:T(8,128)} %bitcast.51, s32[128]{0:T(128)S(1)} %eq.91), kind=kOutput, calls=%fused_computation.17 | convolution fusion | flops 905977856 | bytes 7078400 | tf_op jit(solution)/shard_map/at,tcw->acw/dot_general | solution.py:45
  160.8 2.0 fusion
  162.8 2.7 copy.20
  165.6 109.3 %all_to_all.37 = f32[32,4,24,384]{3,2,1,0:T(8,128)S(1)} all-to-all(f32[32,4,24,384]{3,2,1,0:T(8,128)S(1)} %copy.20), channel_id=1, replica_groups=mesh['gx'=4,'gy'=8] {'gx','gy'}, dimensions={0} | all-to-all | bytes 9437184 | tf_op jit(solution)/shard_map/all_to_all | solution.py:56
  274.9 2.2 copy.28
  (17 shorter events, 0.5 us)
Async XLA Ops:
  0.0 10.9 %copy-start = (bf16[64,24,128]{2,1,0:T(8,128)(2,1)S(1)}, bf16[64,24,128]{2,1,0:T(8,128)(2,1)}, u32[]{:S(2)}) copy-start(bf16[64,24,128]{2,1,0:T(8,128)(2,1)} %param.6) | copy-start | bytes 1179652
  12.5 24.0 %all-to-all-start.2 = ((bf16[128,24,128]{2,1,0:T(8,128)(2,1)}), bf16[128,24,128]{2,1,0:T(8,128)(2,1)S(1)}, u32[]{:S(2)}, u32[]{:S(2)}) async-start(bf16[128,24,128]{2,1,0:T(8,128)(2,1)} %gather_fusion), calls=%async_computation.2 | async-start | bytes 1572864 | tf_op jit(solution)/shard_map/all_to_all | solution.py:24
  36.4 34.1 %all-to-all-start.1 = ((f32[32,4,4]{1,2,0:T(4,128)}), f32[32,4,4]{1,2,0:T(4,128)S(1)}, u32[]{:S(2)}, u32[]{:S(2)}) async-start(f32[32,4,4]{1,2,0:T(4,128)} %copy.13), calls=%async_computation.1 | async-start | bytes 131072 | tf_op jit(solution)/shard_map/all_to_all | solution.py:34
  63.3 13.1 %copy-start.2 = (s32[64,1]{0,1:T(1,128)S(1)}, s32[64,1]{0,1:T(1,128)}, u32[]{:S(2)}) copy-start(s32[64,1]{0,1:T(1,128)} %param.11) | copy-start | bytes 772
  70.5 31.8 %all-to-all-start.3 = ((f32[32,1,9216]{2,1,0:T(1,128)}), f32[32,1,9216]{2,1,0:T(1,128)S(1)}, u32[]{:S(2)}, u32[]{:S(2)}) async-start(f32[32,1,9216]{2,1,0:T(1,128)} %reshape.128), calls=%async_computation.3 | async-start | bytes 2359296 | tf_op jit(solution)/shard_map/all_to_all | solution.py:33
  274.9 2.2 copy-start.1
where the time goes:
time: 282 us; the launch traced here: 277 us
  blocking collectives  119 us (42%)
  local copies, waits for them, and re-layouts  50.6 us (18%)
  matrix products  43.9 us (16%)
  waiting for transfers between devices  39.5 us (14%)
  starting transfers between devices  17.8 us (6%)
  other arithmetic  5.93 us (2%)
    all_to_all x1, blocking collectives, per_device(): lax.all_to_all(outgoing, ('gx', 'gy'), split_axis=0, concat_axis=0, tiled...  109 us
    all_to_all x1, waiting for transfers between devices, per_device(): lax.all_to_all(partial_value, ('gx', 'gy'), split_axis=0, concat_axis=0,...  23.8 us
    dot_general x1, matrix products, placed(): jnp.einsum('tqce,tqn->tcne', partial_value, column_hot, precision=HIGH)  19 us
    unnamed x9, local copies, waits for them, and re-layouts  15.7 us
    all_to_all x1, waiting for transfers between devices, per_device(): lax.all_to_all(prolong[requested], ('gx', 'gy'), split_axis=0, concat_axi...  15.7 us
    transpose x1, local copies, waits for them, and re-layouts, placed(): jnp.einsum('tqce,tqn->tcne', partial_value, column_hot, precision=HIGH)  15.4 us
    dot_general x1, matrix products, per_device(): jnp.einsum('tqij,tqej->tqei', stiffness, col_rows, preferred_element_type...  12.8 us
    all_to_all x1, blocking collectives, per_device(): lax.all_to_all(request, ('gx', 'gy'), split_axis=0, concat_axis=0, tiled=...  9.94 us
  transfers between devices with their start and end apart: 3, of which 2 were waited for; matrix products, arithmetic and copies ran while one was open for 12% of the time, Pallas kernels for 0%

commit v1 on v0

v1 whole, which is shorter than its diff:
```python
import functools

import jax
import jax.numpy as jnp
from jax import lax
from jax.experimental import pallas as pl
from jax.experimental.pallas import tpu as pltpu
from jax.sharding import PartitionSpec as P

MAXNB = 16
AXES = ("gx", "gy")
LANES = 128
TOP = 32767.0
MESH = pl.DeviceIdType.MESH
HBM = pl.BlockSpec(memory_space=pl.ANY)
VMEM = pl.BlockSpec(memory_space=pltpu.VMEM)
SMEM = pl.BlockSpec(memory_space=pltpu.SMEM)
NT = (((1,), (1,)), ((), ()))


def exchange_kernel(gx, gy, count, *refs):
    ins, outs = refs[:count], refs[count : 2 * count]
    send_sem, recv_sem, local_sem = refs[2 * count :]
    n = gx * gy
    me = lax.axis_index("gx") * gy + lax.axis_index("gy")
    barrier = pltpu.get_barrier_semaphore()

    def greet(k, c):
        peer = lax.rem(me + k, n)
        pl.semaphore_signal(barrier, inc=1, device_id=(peer // gy, lax.rem(peer, gy)), device_id_type=MESH)
        return c

    lax.fori_loop(1, n, greet, 0)
    own = [pltpu.make_async_copy(ins[i].at[me], outs[i].at[me], local_sem.at[i]) for i in range(count)]
    for copy in own:
        copy.start()
    pl.semaphore_wait(barrier, n - 1)

    def copies(k, source):
        peer = lax.rem(me + k, n)
        return [
            pltpu.make_async_remote_copy(
                src_ref=ins[i].at[peer],
                dst_ref=outs[i].at[source],
                send_sem=send_sem.at[i, k],
                recv_sem=recv_sem.at[i, k],
                device_id=(peer // gy, lax.rem(peer, gy)),
                device_id_type=MESH,
            )
            for i in range(count)
        ]

    def send(k, c):
        for copy in copies(k, me):
            copy.start()
        return c

    lax.fori_loop(1, n, send, 0)

    def drain(k, c):
        for copy in copies(k, lax.rem(me + n - k, n)):
            copy.wait()
        return c

    lax.fori_loop(1, n, drain, 0)
    for copy in own:
        copy.wait()


def exchange(arrays, gx, gy, number):
    count = len(arrays)
    n = gx * gy
    return pl.pallas_call(
        functools.partial(exchange_kernel, gx, gy, count),
        out_shape=[jax.ShapeDtypeStruct(a.shape, a.dtype) for a in arrays],
        in_specs=[HBM] * count,
        out_specs=[HBM] * count,
        scratch_shapes=[
            pltpu.SemaphoreType.DMA((count, n)),
            pltpu.SemaphoreType.DMA((count, n)),
            pltpu.SemaphoreType.DMA((count,)),
        ],
        compiler_params=pltpu.CompilerParams(collective_id=number, has_side_effects=True),
        name=f"exchange{number}",
    )(*arrays)


def as_row(column):
    rows = column.shape[0]
    shape = (rows, LANES)
    eye = lax.broadcasted_iota(jnp.int32, shape, 0) == lax.broadcasted_iota(jnp.int32, shape, 1)
    return jnp.sum(jnp.where(eye, column, 0.0), axis=0, keepdims=True)


def as_column(row, rows):
    shape = (rows, LANES)
    eye = lax.broadcasted_iota(jnp.int32, shape, 0) == lax.broadcasted_iota(jnp.int32, shape, 1)
    return jnp.sum(jnp.where(eye, row, 0.0), axis=1, keepdims=True)


def coded(values):
    top = jnp.maximum(jnp.max(jnp.abs(values), axis=1, keepdims=True), 1e-30)
    code = jnp.round(values * (TOP / top)).astype(jnp.int32).astype(jnp.int16)
    return code, as_row(top * (1.0 / TOP))


def product_kernel(dims, slot_ref, fetched_ref, stiff_ref, *refs):
    cv, bps, group, per_step, quant = dims
    if quant:
        out_ref, scale_ref, wide_ref, cols_ref = refs
    else:
        out_ref, wide_ref, cols_ref = refs
    dof = stiff_ref.shape[-1]
    step = pl.program_id(0)
    span = bps * cv

    @pl.when(step == 0)
    def _():
        wide_ref[...] = fetched_ref[...].astype(jnp.float32)

    lane = lax.broadcasted_iota(jnp.int32, (dof, LANES), 1)

    def body(k, c):
        grp = step * per_step + k
        applied = []
        for tl in range(group):
            for q in range(bps):
                block = wide_ref[slot_ref[(grp * group + tl) * bps + q]]
                at = (span * tl + cv * q) % LANES
                first = min(cv, LANES - at)
                cols_ref[tl, at : at + first, :] = block[:first]
                if first < cv:
                    cols_ref[tl, 0 : cv - first, :] = block[first:]
            cols = cols_ref[tl].astype(jnp.bfloat16)
            mats = stiff_ref[k * group + tl].reshape(bps * dof, dof)
            prod = lax.dot_general(mats, cols, NT, preferred_element_type=jnp.float32)
            rel = (lane + (LANES * tl - span * tl) % LANES) % LANES
            one = prod[(bps - 1) * dof :]
            for q in range(bps - 2, -1, -1):
                one = jnp.where(rel < cv * (q + 1), prod[q * dof : (q + 1) * dof], one)
            applied.append(one)
        tiles = []
        for j in range(span * group // LANES):
            low, high = LANES * j // span, (LANES * (j + 1) - 1) // span
            tile = applied[high]
            for tl in range(high - 1, low - 1, -1):
                tile = jnp.where(lane < span * (tl + 1) - LANES * j, applied[tl], tile)
            tiles.append(tile)
        whole = jnp.concatenate(tiles, axis=1)
        hi = whole.astype(jnp.bfloat16)
        lo = (whole - hi.astype(jnp.float32)).astype(jnp.bfloat16)
        rows = wide_ref[pl.ds(grp * group, group)].reshape(group * cv, dof).astype(jnp.bfloat16)
        both = jnp.dot(rows, hi, preferred_element_type=jnp.float32) + jnp.dot(
            rows, lo, preferred_element_type=jnp.float32
        )
        wide_lane = lax.broadcasted_iota(jnp.int32, (cv, span * group), 1)
        out = both[(group - 1) * cv :]
        for tl in range(group - 2, -1, -1):
            out = jnp.where(wide_lane < span * (tl + 1), both[tl * cv : (tl + 1) * cv], out)
        if quant:
            out_ref[k], scale_ref[k] = coded(out)
        else:
            out_ref[k] = out
        return c

    lax.fori_loop(0, per_step, body, 0)


def products(fetched, stiffness, col_slot, group, quant):
    slots, cv, dof = fetched.shape
    bps = stiffness.shape[1]
    groups = slots // group
    per_step = 4 if groups % 4 == 0 else 1
    width = group * bps * cv
    out_shape = [jax.ShapeDtypeStruct((groups, cv, width), jnp.int16 if quant else jnp.float32)]
    out_specs = [pl.BlockSpec((per_step, cv, width), lambda i: (i, 0, 0))]
    if quant:
        out_shape.append(jax.ShapeDtypeStruct((groups, 1, LANES), jnp.float32))
        out_specs.append(pl.BlockSpec((per_step, 1, LANES), lambda i: (i, 0, 0)))
    return pl.pallas_call(
        functools.partial(product_kernel, (cv, bps, group, per_step, quant)),
        grid=(groups // per_step,),
        out_shape=out_shape,
        in_specs=[
            SMEM,
            pl.BlockSpec((slots, cv, dof), lambda i: (0, 0, 0)),
            pl.BlockSpec((per_step * group, bps, dof, dof), lambda i: (i, 0, 0, 0)),
        ],
        out_specs=out_specs,
        scratch_shapes=[
            pltpu.VMEM((slots, cv, dof), jnp.float32),
            pltpu.VMEM((group, LANES, dof), jnp.float32),
        ],
        compiler_params=pltpu.CompilerParams(vmem_limit_bytes=48 << 20),
        name="products",
    )(col_slot.reshape(-1), fetched, stiffness)


def gather_rows_kernel(dims, req_ref, owner_ref, target_ref, part_ref, *refs):
    cv, group, send_max, quant = dims
    if quant:
        scale_ref, out_ref, out_scale_ref, total_ref, place_ref, seen_ref = refs
    else:
        out_ref, out_scale_ref, total_ref, place_ref, seen_ref = refs
    n = out_ref.shape[0]
    groups, _, width = part_ref.shape
    span = width // group
    total_ref[...] = jnp.zeros_like(total_ref)

    def clear(i, c):
        seen_ref[i] = 0
        return c

    lax.fori_loop(0, n, clear, 0)

    def rank(a, c):
        owner = owner_ref[a]
        before = seen_ref[owner]
        place_ref[a] = owner * send_max + before
        seen_ref[owner] = before + 1
        return c

    lax.fori_loop(0, owner_ref.shape[0], rank, 0)
    lane = lax.broadcasted_iota(jnp.int32, (cv, width), 1)
    column = lax.broadcasted_iota(jnp.int32, (width, width), 0)

    def body(g, c):
        hot = jnp.where(column == target_ref[g], 1.0, 0.0).astype(jnp.bfloat16)
        if quant:
            code = part_ref[g].astype(jnp.int32)
            high = code >> 8
            pieces = [high.astype(jnp.float32), (code - high * 256).astype(jnp.float32)]
            weights = [256.0, 1.0]
        else:
            rest = part_ref[g]
            pieces, weights = [], [1.0, 1.0, 1.0]
            for _ in range(3):
                piece = rest.astype(jnp.bfloat16).astype(jnp.float32)
                pieces.append(piece)
                rest = rest - piece
        placed = 0.0
        for piece, weight in zip(pieces, weights):
            stack = jnp.concatenate(
                [
                    jnp.where((lane >= span * tl) & (lane < span * (tl + 1)), piece, 0.0)
                    for tl in range(group)
                ],
                axis=0,
            ).astype(jnp.bfloat16)
            placed = placed + weight * lax.dot_general(
                stack, hot, NT, preferred_element_type=jnp.float32
            )
        if quant:
            factor = as_column(scale_ref[g], cv)
        for tl in range(group):
            where = place_ref[req_ref[g * group + tl]]
            rows = placed[tl * cv : (tl + 1) * cv]
            if quant:
                rows = rows * factor
            total_ref[where] = total_ref[where] + rows
        return c

    lax.fori_loop(0, groups, body, 0)

    def emit(p, c):
        rows = total_ref[pl.ds(p * send_max, send_max)].reshape(send_max * cv, width)
        out_ref[p], out_scale_ref[p] = coded(rows)
        return c

    lax.fori_loop(0, n, emit, 0)


def gathered_rows(part, scale, target, requested, owners, n, send_max, group):
    groups, cv, width = part.shape
    quant = scale is not None
    args = [requested, owners, target, part] + ([scale] if quant else [])
    return pl.pallas_call(
        functools.partial(gather_rows_kernel, (cv, group, send_max, quant)),
        out_shape=[
            jax.ShapeDtypeStruct((n, send_max * cv, width), jnp.int16),
            jax.ShapeDtypeStruct((n, 1, LANES), jnp.float32),
        ],
        in_specs=[SMEM, SMEM] + [VMEM] * (len(args) - 2),
        out_specs=[VMEM, VMEM],
        scratch_shapes=[
            pltpu.VMEM((n * send_max, cv, width), jnp.float32),
            pltpu.SMEM((owners.shape[0],), jnp.int32),
            pltpu.SMEM((n,), jnp.int32),
        ],
        compiler_params=pltpu.CompilerParams(vmem_limit_bytes=48 << 20),
        name="gathered_rows",
    )(*args)


def decode_kernel(cv, code_ref, scale_ref, out_ref):
    per_step, rows, width = code_ref.shape

    for p in range(per_step):
        values = code_ref[p].astype(jnp.int32).astype(jnp.float32) * as_column(scale_ref[p], rows)
        out_ref[p * (rows // cv) : (p + 1) * (rows // cv)] = values.reshape(rows // cv, cv, width)


def decoded(code, scale, cv):
    n, rows, width = code.shape
    per_step = 4 if n % 4 == 0 else 1
    return pl.pallas_call(
        functools.partial(decode_kernel, cv),
        grid=(n // per_step,),
        out_shape=jax.ShapeDtypeStruct((n * rows // cv, cv, width), jnp.float32),
        in_specs=[
            pl.BlockSpec((per_step, rows, width), lambda i: (i, 0, 0)),
            pl.BlockSpec((per_step, 1, LANES), lambda i: (i, 0, 0)),
        ],
        out_specs=pl.BlockSpec((per_step * rows // cv, cv, width), lambda i: (i, 0, 0)),
        name="decoded",
    )(code, scale)


def per_device(gx, gy, prolong, stiffness, request, col_slot, col_pos, coarse_owner):
    n = gx * gy
    own_aggs, cv, dof = prolong.shape
    slots, bps = col_slot.shape
    per_peer = slots // n
    group = MAXNB // bps
    quant = per_peer == group
    send_max = (2 * own_aggs + n - 1) // n

    meta = jnp.concatenate([request.reshape(n, per_peer), col_pos.reshape(n, per_peer * bps)], axis=1)
    meta = jnp.pad(meta, ((0, 0), (0, LANES - meta.shape[1])))[:, None, :]
    (meta_in,) = exchange([meta], gx, gy, 1)
    requested = meta_in[:, 0, :per_peer].reshape(-1)
    pos_in = meta_in[:, 0, per_peer : per_peer * (1 + bps)].reshape(slots // group, group * bps)
    target = (cv * pos_in[:, :, None] + jnp.arange(cv, dtype=jnp.int32)).reshape(
        slots // group, 1, group * bps * cv
    )
    answer = prolong[requested].reshape(n, per_peer * cv, dof)
    (fetched,) = exchange([answer], gx, gy, 2)
    fetched = fetched.reshape(slots, cv, dof)
    made = products(fetched, stiffness, col_slot, group, quant)
    if quant:
        part, scale = exchange(made, gx, gy, 3)
    else:
        flat = made[0].reshape(slots // group, cv, group, bps * cv).transpose(0, 2, 1, 3)
        (flat,) = exchange([flat.reshape(n, per_peer * cv, bps * cv)], gx, gy, 3)
        flat = flat.reshape(slots // group, group, cv, bps * cv).transpose(0, 2, 1, 3)
        part, scale = flat.reshape(slots // group, cv, group * bps * cv), None
    code, factor = gathered_rows(
        part, scale, target, requested, coarse_owner[:, 0], n, send_max, group
    )
    code, factor = exchange([code, factor], gx, gy, 4)
    return decoded(code, factor, cv)


def solution(mesh):
    gx, gy = mesh.shape["gx"], mesh.shape["gy"]
    placed = (
        P(AXES, None, None),
        P(AXES, None, None, None),
        P(AXES),
        P(AXES, None),
        P(AXES, None),
        P(AXES, None),
    )
    return jax.shard_map(
        functools.partial(per_device, gx, gy),
        mesh=mesh,
        in_specs=placed,
        out_specs=P(AXES, None, None),
        check_vma=False,
    )
```

time: 282 us -> 172 us (0.61); the launches traced: 277 us -> 172 us
  Pallas kernels: 0 us -> 158 us
  blocking collectives: 119 us -> 0 us
  matrix products: 43.9 us -> 0 us
  waiting for transfers between devices: 39.5 us -> 0 us
  local copies, waits for them, and re-layouts: 50.6 us -> 12.5 us
  starting transfers between devices: 17.8 us -> 0 us
  other arithmetic: 5.93 us -> 0.94 us
    pallas_call x0 -> x7, Pallas kernels: none -> 158 us  [the longest x4 115 us: exchange(): pl.pallas_call(functools.partial(exchange_kernel, gx, gy, count), out_sha...]
    all_to_all x2 -> x0, blocking collectives: 119 us -> none  [the longest x1 109 us: per_device(): lax.all_to_all(outgoing, ('gx', 'gy'), split_axis=0, concat_axis=0, tiled...]
    dot_general x5 -> x0, matrix products: 43.9 us -> none  [the longest x1 19 us: placed(): jnp.einsum('tqce,tqn->tcne', partial_value, column_hot, precision=HIGH)]
    all_to_all x3 -> x0, waiting for transfers between devices: 39.5 us -> none  [the longest x1 23.8 us: per_device(): lax.all_to_all(partial_value, ('gx', 'gy'), split_axis=0, concat_axis=0,...]
    all_to_all x3 -> x0, starting transfers between devices: 17.8 us -> none  [the longest x1 6.06 us: per_device(): lax.all_to_all(col_pos.astype(jnp.float32), ('gx', 'gy'), split_axis=0, c...]
    transpose x1 -> x0, local copies, waits for them, and re-layouts: 15.4 us -> none  [placed(): jnp.einsum('tqce,tqn->tcne', partial_value, column_hot, precision=HIGH)]
    all_to_all x7 -> x0, local copies, waits for them, and re-layouts: 11.4 us -> none  [the longest x2 9.11 us: per_device(): lax.all_to_all(partial_value, ('gx', 'gy'), split_axis=0, concat_axis=0,...]
    unnamed x9 -> x20, local copies, waits for them, and re-layouts: 15.7 us -> 7.9 us
  transfers between devices with their start and end apart: 3 -> 0, of which waited for: 2 -> 0; matrix products, arithmetic and copies ran while one was open for 12% -> 0% of each run, Pallas kernels for 0% -> 0%
where the time goes in v1:
time: 172 us
  Pallas kernels  158 us (92%)
  local copies, waits for them, and re-layouts  12.5 us (7%)
    pallas_call x4, Pallas kernels, exchange(): pl.pallas_call(functools.partial(exchange_kernel, gx, gy, count), out_sha...  115 us
    pallas_call x1, Pallas kernels, products(): pl.pallas_call(functools.partial(product_kernel, (cv, bps, group, per_ste...  20.7 us
    pallas_call x1, Pallas kernels, gathered_rows(): pl.pallas_call(functools.partial(gather_rows_kernel, (cv, group, send_max...  16.1 us
    unnamed x20, local copies, waits for them, and re-layouts  7.9 us
    pallas_call x1, Pallas kernels, decoded(): pl.pallas_call(functools.partial(decode_kernel, cv), grid=(n // per_step,...  6.5 us

profile of v1, /device:TPU:15, one launch (start us, length us, event | category | flops | bytes accessed | tf_op | source)
XLA Modules:
  0.0 171.8 jit_solution(7989969896828565281)
XLA Ops:
  0.0 0.0 copy-start
  0.0 0.1 add.44
  0.1 0.8 reshape.87
  0.9 0.8 copy.14
  1.7 0.1 reshape.89.slot_ref
  1.8 0.8 copy.11
  2.6 0.1 reshape.88
  2.7 0.1 pad_add_fusion
  2.7 0.6 pad.4
  3.4 8.3 %exchange1.1 = s32[32,1,128]{2,1,0:T(1,128)} custom-call(s32[32,1,128]{2,1,0:T(1,128)} %bitcast.13), custom_call_target="tpu_custom_call" | custom-call | tf_op jit(solution)/shard_map/exchange1/pallas_call | solution.py:73
  11.7 0.8 slice_multiply_fusion
  12.5 0.8 fusion.1
  13.3 0.1 reshape_squeeze.6
  13.4 0.1 reshape_squeeze.5.req_ref
  13.5 0.1 add.41
  13.7 0.2 add.49
  13.9 1.6 gather_fusion
  15.5 23.9 %exchange2.1 = bf16[32,96,128]{2,1,0:T(8,128)(2,1)} custom-call(bf16[32,96,128]{2,1,0:T(8,128)(2,1)} %bitcast.10), custom_call_target="tpu_custom_call" | custom-call | tf_op jit(solution)/shard_map/exchange2/pallas_call | solution.py:73
  39.4 1.1 copy-done.1
  40.5 20.7 %products.1 = (s16[32,24,384]{2,1,0:T(8,128)(2,1)S(1)}, f32[32,1,128]{2,1,0:T(1,128)S(1)}) custom-call(s32[512]{0:T(512)S(1)} %reshape.89.slot_ref, bf16[128,24,128]{2,1,0:T(8,128)(2,1)S(1)} %bitcast.8, bf16[128,4,128,128]{3,2,1,0:T(8,128)(2,1)} %stiff_ref.1), custom_call_target="tpu_custom_call" | custom-call | tf_op jit(solution)/shard_map/products/pallas_call | solution.py:180
  61.2 0.0 copy-start.4
  61.2 0.8 copy-done.4
  62.0 0.6 copy-done.7
  62.6 19.9 %exchange3.1 = (s16[32,24,384]{2,1,0:T(8,128)(2,1)}, f32[32,1,128]{2,1,0:T(1,128)}) custom-call(s16[32,24,384]{2,1,0:T(8,128)(2,1)} %copy-done.4, f32[32,1,128]{2,1,0:T(1,128)} %copy-done.7), custom_call_target="tpu_custom_call" | custom-call | tf_op jit(solution)/shard_map/exchange3/pallas_call | solution.py:73
  82.5 1.1 copy-done.3
  83.5 0.7 copy-done.6
  84.3 16.1 %gathered_rows.1 = (s16[32,96,384]{2,1,0:T(8,128)(2,1)S(1)}, f32[32,1,128]{2,1,0:T(1,128)S(1)}) custom-call(s32[128]{0:T(128)S(1)} %reshape_squeeze.5.req_ref, s32[64]{0:T(128)S(1)} %bitcast.9, s32[32,1,384]{2,1,0:T(1,128)S(1)} %broadcast_add_fusion.target_ref, s16[32,24,384]{2,1,0:T(8,128)(2,1)S(1)} %copy-done.3, f32[32,1,128]{2,1,0:T(1,128)S(1)} %copy-done.6), custom_call_target="tpu_custom_call" | custom-call | tf_op jit(solution)/shard_map/gathered_rows/pallas_call | solution.py:277
  100.3 0.0 copy-start.2
  100.3 1.4 copy-done.2
  101.7 0.6 copy-done.5
  102.3 62.9 %exchange4.1 = (s16[32,96,384]{2,1,0:T(8,128)(2,1)}, f32[32,1,128]{2,1,0:T(1,128)}) custom-call(s16[32,96,384]{2,1,0:T(8,128)(2,1)} %copy-done.2, f32[32,1,128]{2,1,0:T(1,128)} %copy-done.5), custom_call_target="tpu_custom_call" | custom-call | tf_op jit(solution)/shard_map/exchange4/pallas_call | solution.py:73
  165.3 6.5 %decoded.1 = f32[128,24,384]{2,1,0:T(8,128)} custom-call(s16[32,96,384]{2,1,0:T(8,128)(2,1)} %get-tuple-element.19.code_ref, f32[32,1,128]{2,1,0:T(1,128)} %get-tuple-element.20.scale_ref), custom_call_target="tpu_custom_call" | custom-call | tf_op jit(solution)/shard_map/decoded/pallas_call | solution.py:306
  (12 shorter events, 0.1 us)
Async XLA Ops:
  0.0 13.9 %copy-start = (bf16[64,24,128]{2,1,0:T(8,128)(2,1)S(1)}, bf16[64,24,128]{2,1,0:T(8,128)(2,1)}, u32[]{:S(2)}) copy-start(bf16[64,24,128]{2,1,0:T(8,128)(2,1)} %param.6) | copy-start | bytes 1179652
  39.4 1.1 copy-start.1
  40.5 42.0 %copy-start.8 = (s32[64,1]{0,1:T(1,128)S(1)}, s32[64,1]{0,1:T(1,128)}, u32[]{:S(2)}) copy-start(s32[64,1]{0,1:T(1,128)} %param.11) | copy-start | bytes 772
  61.2 0.8 copy-start.4
  62.0 0.6 copy-start.7
  82.5 1.1 copy-start.3
  83.5 0.7 copy-start.6
  100.3 1.4 copy-start.2
  101.7 0.6 copy-start.5

commit v2 on v1

--- a/solution.py
+++ b/solution.py
@@ -104,89 +104,84 @@
     return code, as_row(top * (1.0 / TOP))
 
 
-def product_kernel(dims, slot_ref, fetched_ref, stiff_ref, *refs):
-    cv, bps, group, per_step, quant = dims
-    if quant:
-        out_ref, scale_ref, wide_ref, cols_ref = refs
-    else:
-        out_ref, wide_ref, cols_ref = refs
-    dof = stiff_ref.shape[-1]
+def group_product(dims, grp, slot_ref, wide_ref, cols_ref, mats_of):
+    cv, bps, group = dims
+    dof = wide_ref.shape[-1]
+    span = bps * cv
+    lane = lax.broadcasted_iota(jnp.int32, (dof, LANES), 1)
+    applied = []
+    for tl in range(group):
+        for q in range(bps):
+            block = wide_ref[slot_ref[(grp * group + tl) * bps + q]]
+            at = (span * tl + cv * q) % LANES
+            first = min(cv, LANES - at)
+            cols_ref[tl, at : at + first, :] = block[:first]
+            if first < cv:
+                cols_ref[tl, 0 : cv - first, :] = block[first:]
+    for tl in range(group):
+        cols = cols_ref[tl].astype(jnp.bfloat16)
+        mats = mats_of(tl).reshape(bps * dof, dof)
+        prod = lax.dot_general(mats, cols, NT, preferred_element_type=jnp.float32)
+        rel = (lane + (LANES * tl - span * tl) % LANES) % LANES
+        one = prod[(bps - 1) * dof :]
+        for q in range(bps - 2, -1, -1):
+            one = jnp.where(rel < cv * (q + 1), prod[q * dof : (q + 1) * dof], one)
+        applied.append(one)
+    tiles = []
+    for j in range(span * group // LANES):
+        low, high = LANES * j // span, (LANES * (j + 1) - 1) // span
+        tile = applied[high]
+        for tl in range(high - 1, low - 1, -1):
+            tile = jnp.where(lane < span * (tl + 1) - LANES * j, applied[tl], tile)
+        tiles.append(tile)
+    whole = jnp.concatenate(tiles, axis=1)
+    hi = whole.astype(jnp.bfloat16)
+    lo = (whole - hi.astype(jnp.float32)).astype(jnp.bfloat16)
+    rows = wide_ref[pl.ds(grp * group, group)].reshape(group * cv, dof).astype(jnp.bfloat16)
+    both = jnp.dot(rows, hi, preferred_element_type=jnp.float32) + jnp.dot(
+        rows, lo, preferred_element_type=jnp.float32
+    )
+    wide_lane = lax.broadcasted_iota(jnp.int32, (cv, span * group), 1)
+    out = both[(group - 1) * cv :]
+    for tl in range(group - 2, -1, -1):
+        out = jnp.where(wide_lane < span * (tl + 1), both[tl * cv : (tl + 1) * cv], out)
+    return out
+
+
+def product_kernel(dims, slot_ref, fetched_ref, stiff_ref, out_ref, wide_ref, cols_ref):
+    cv, bps, group, per_step = dims
     step = pl.program_id(0)
-    span = bps * cv
 
     @pl.when(step == 0)
     def _():
         wide_ref[...] = fetched_ref[...].astype(jnp.float32)
 
-    lane = lax.broadcasted_iota(jnp.int32, (dof, LANES), 1)
-
     def body(k, c):
-        grp = step * per_step + k
-        applied = []
-        for tl in range(group):
-            for q in range(bps):
-                block = wide_ref[slot_ref[(grp * group + tl) * bps + q]]
-                at = (span * tl + cv * q) % LANES
-                first = min(cv, LANES - at)
-                cols_ref[tl, at : at + first, :] = block[:first]
-                if first < cv:
-                    cols_ref[tl, 0 : cv - first, :] = block[first:]
-            cols = cols_ref[tl].astype(jnp.bfloat16)
-            mats = stiff_ref[k * group + tl].reshape(bps * dof, dof)
-            prod = lax.dot_general(mats, cols, NT, preferred_element_type=jnp.float32)
-            rel = (lane + (LANES * tl - span * tl) % LANES) % LANES
-            one = prod[(bps - 1) * dof :]
-            for q in range(bps - 2, -1, -1):
-                one = jnp.where(rel < cv * (q + 1), prod[q * dof : (q + 1) * dof], one)
-            applied.append(one)
-        tiles = []
-        for j in range(span * group // LANES):
-            low, high = LANES * j // span, (LANES * (j + 1) - 1) // span
-            tile = applied[high]
-            for tl in range(high - 1, low - 1, -1):
-                tile = jnp.where(lane < span * (tl + 1) - LANES * j, applied[tl], tile)
-            tiles.append(tile)
-        whole = jnp.concatenate(tiles, axis=1)
-        hi = whole.astype(jnp.bfloat16)
-        lo = (whole - hi.astype(jnp.float32)).astype(jnp.bfloat16)
-        rows = wide_ref[pl.ds(grp * group, group)].reshape(group * cv, dof).astype(jnp.bfloat16)
-        both = jnp.dot(rows, hi, preferred_element_type=jnp.float32) + jnp.dot(
-            rows, lo, preferred_element_type=jnp.float32
+        out_ref[k] = group_product(
+            (cv, bps, group), step * per_step + k, slot_ref, wide_ref, cols_ref,
+            lambda tl: stiff_ref[k * group + tl],
         )
-        wide_lane = lax.broadcasted_iota(jnp.int32, (cv, span * group), 1)
-        out = both[(group - 1) * cv :]
-        for tl in range(group - 2, -1, -1):
-            out = jnp.where(wide_lane < span * (tl + 1), both[tl * cv : (tl + 1) * cv], out)
-        if quant:
-            out_ref[k], scale_ref[k] = coded(out)
-        else:
-            out_ref[k] = out
         return c
 
     lax.fori_loop(0, per_step, body, 0)
 
 
-def products(fetched, stiffness, col_slot, group, quant):
+def products(fetched, stiffness, col_slot, group):
     slots, cv, dof = fetched.shape
     bps = stiffness.shape[1]
     groups = slots // group
     per_step = 4 if groups % 4 == 0 else 1
     width = group * bps * cv
-    out_shape = [jax.ShapeDtypeStruct((groups, cv, width), jnp.int16 if quant else jnp.float32)]
-    out_specs = [pl.BlockSpec((per_step, cv, width), lambda i: (i, 0, 0))]
-    if quant:
-        out_shape.append(jax.ShapeDtypeStruct((groups, 1, LANES), jnp.float32))
-        out_specs.append(pl.BlockSpec((per_step, 1, LANES), lambda i: (i, 0, 0)))
     return pl.pallas_call(
-        functools.partial(product_kernel, (cv, bps, group, per_step, quant)),
+        functools.partial(product_kernel, (cv, bps, group, per_step)),
         grid=(groups // per_step,),
-        out_shape=out_shape,
+        out_shape=jax.ShapeDtypeStruct((groups, cv, width), jnp.float32),
         in_specs=[
             SMEM,
             pl.BlockSpec((slots, cv, dof), lambda i: (0, 0, 0)),
             pl.BlockSpec((per_step * group, bps, dof, dof), lambda i: (i, 0, 0, 0)),
         ],
-        out_specs=out_specs,
+        out_specs=pl.BlockSpec((per_step, cv, width), lambda i: (i, 0, 0)),
         scratch_shapes=[
             pltpu.VMEM((slots, cv, dof), jnp.float32),
             pltpu.VMEM((group, LANES, dof), jnp.float32),
@@ -196,8 +191,178 @@
     )(col_slot.reshape(-1), fetched, stiffness)
 
 
-def gather_rows_kernel(dims, req_ref, owner_ref, target_ref, part_ref, *refs):
-    cv, group, send_max, quant = dims
+def fused_kernel(
+    dims,
+    slot_ref, meta_ref, prolong_ref, stiff_ref,
+    meta_out, part_out, scale_out,
+    req_ref, stage_ref, fetched_ref, wide_ref, cols_ref, mats_ref, code_ref, factor_ref,
+    meta_send, meta_recv, fetch_send, fetch_recv, part_send, part_recv, scale_send, scale_recv,
+    mats_sem, own_sem,
+):
+    gx, gy, cv, bps, group = dims
+    n = gx * gy
+    me = lax.axis_index("gx") * gy + lax.axis_index("gy")
+    barrier = pltpu.get_barrier_semaphore()
+
+    def where(peer):
+        return (peer // gy, lax.rem(peer, gy))
+
+    def remote(src, dst, send_sem, recv_sem, peer):
+        return pltpu.make_async_remote_copy(
+            src_ref=src, dst_ref=dst, send_sem=send_sem, recv_sem=recv_sem,
+            device_id=where(peer), device_id_type=MESH,
+        )
+
+    def meta_copy(k, peer, source):
+        return remote(meta_ref.at[peer], meta_out.at[source], meta_send.at[k], meta_recv.at[k], peer)
+
+    def fetch_copy(k, peer, source):
+        return remote(
+            stage_ref.at[pl.ds(peer * group, group)],
+            fetched_ref.at[pl.ds(source * group, group)],
+            fetch_send.at[k], fetch_recv.at[k], peer,
+        )
+
+    def part_copies(k, peer, source):
+        return (
+            remote(code_ref.at[peer], part_out.at[source], part_send.at[k], part_recv.at[k], peer),
+            remote(factor_ref.at[peer], scale_out.at[source], scale_send.at[k], scale_recv.at[k], peer),
+        )
+
+    def mats_copy(peer):
+        return pltpu.make_async_copy(
+            stiff_ref.at[pl.ds(peer * group, group)],
+            mats_ref.at[pl.ds(peer * group, group)],
+            mats_sem.at[peer],
+        )
+
+    def greet(k, c):
+        pl.semaphore_signal(barrier, inc=1, device_id=where(lax.rem(me + k, n)), device_id_type=MESH)
+        return c
+
+    lax.fori_loop(1, n, greet, 0)
+    own_meta = pltpu.make_async_copy(meta_ref.at[me], meta_out.at[me], own_sem.at[0])
+    own_meta.start()
+
+    def load(k, c):
+        mats_copy(lax.rem(me + k, n)).start()
+        return c
+
+    lax.fori_loop(1, n + 1, load, 0)
+    pl.semaphore_wait(barrier, n - 1)
+
+    def ask(k, c):
+        meta_copy(k, lax.rem(me + k, n), me).start()
+        return c
+
+    lax.fori_loop(1, n, ask, 0)
+    own_meta.wait()
+
+    def asked(k, c):
+        meta_copy(k, lax.rem(me + n - k, n), lax.rem(me + n - k, n)).wait()
+        return c
+
+    lax.fori_loop(1, n, asked, 0)
+    to_scalars = pltpu.make_async_copy(meta_out, req_ref, own_sem.at[1])
+    to_scalars.start()
+    to_scalars.wait()
+
+    def fill(k, c):
+        peer = lax.rem(me + k, n)
+        for j in range(group):
+            stage_ref[peer * group + j] = prolong_ref[req_ref[peer, 0, j]]
+        return c
+
+    lax.fori_loop(1, n + 1, fill, 0)
+
+    def answer(k, c):
+        fetch_copy(k, lax.rem(me + k, n), me).start()
+        return c
+
+    lax.fori_loop(1, n, answer, 0)
+    for j in range(group):
+        wide_ref[me * group + j] = stage_ref[me * group + j].astype(jnp.float32)
+
+    def take(k, c):
+        source = lax.rem(me + n - k, n)
+        fetch_copy(k, source, source).wait()
+        for j in range(group):
+            wide_ref[source * group + j] = fetched_ref[source * group + j].astype(jnp.float32)
+        return c
+
+    lax.fori_loop(1, n, take, 0)
+
+    def work(k, c):
+        peer = lax.rem(me + k, n)
+        mats_copy(peer).wait()
+        out = group_product(
+            (cv, bps, group), peer, slot_ref, wide_ref, cols_ref,
+            lambda tl: mats_ref[peer * group + tl],
+        )
+        code_ref[peer], factor_ref[peer] = coded(out)
+
+        @pl.when(k > 1)
+        def _():
+            for copy in part_copies(k - 1, lax.rem(me + k - 1, n), me):
+                copy.start()
+
+        return c
+
+    lax.fori_loop(1, n + 1, work, 0)
+    own = (
+        pltpu.make_async_copy(code_ref.at[me], part_out.at[me], own_sem.at[2]),
+        pltpu.make_async_copy(factor_ref.at[me], scale_out.at[me], own_sem.at[3]),
+    )
+    for copy in own:
+        copy.start()
+
+    def drain(k, c):
+        source = lax.rem(me + n - k, n)
+        for copy in part_copies(k, source, source):
+            copy.wait()
+        return c
+
+    lax.fori_loop(1, n, drain, 0)
+    for copy in own:
+        copy.wait()
+
+
+def fused(meta, prolong, stiffness, col_slot, gx, gy, group):
+    slots, bps, dof, _ = stiffness.shape
+    cv = prolong.shape[1]
+    n = gx * gy
+    width = group * bps * cv
+    sem = pltpu.SemaphoreType.DMA
+    return pl.pallas_call(
+        functools.partial(fused_kernel, (gx, gy, cv, bps, group)),
+        out_shape=[
+            jax.ShapeDtypeStruct(meta.shape, jnp.int32),
+            jax.ShapeDtypeStruct((n, cv, width), jnp.int16),
+            jax.ShapeDtypeStruct((n, 1, LANES), jnp.float32),
+        ],
+        in_specs=[SMEM, VMEM, VMEM, HBM],
+        out_specs=[VMEM, VMEM, VMEM],
+        scratch_shapes=[
+            pltpu.SMEM(meta.shape, jnp.int32),
+            pltpu.VMEM((slots, cv, dof), jnp.bfloat16),
+            pltpu.VMEM((slots, cv, dof), jnp.bfloat16),
+            pltpu.VMEM((slots, cv, dof), jnp.float32),
+            pltpu.VMEM((group, LANES, dof), jnp.float32),
+            pltpu.VMEM((slots, bps, dof, dof), jnp.bfloat16),
+            pltpu.VMEM((n, cv, width), jnp.int16),
+            pltpu.VMEM((n, 1, LANES), jnp.float32),
+        ]
+        + [sem((n,))] * 9
+        + [sem((4,))],
+        compiler_params=pltpu.CompilerParams(
+            collective_id=1, has_side_effects=True, vmem_limit_bytes=56 << 20
+        ),
+        name="fused",
+    )(col_slot.reshape(-1), meta, prolong, stiffness)
+
+
+def gather_rows_kernel(dims, meta_ref, owner_ref, part_ref, *refs):
+    cv, bps, per_peer, group, send_max, quant = dims
     if quant:
         scale_ref, out_ref, out_scale_ref, total_ref, place_ref, seen_ref = refs
     else:
@@ -223,9 +388,15 @@
     lax.fori_loop(0, owner_ref.shape[0], rank, 0)
     lane = lax.broadcasted_iota(jnp.int32, (cv, width), 1)
     column = lax.broadcasted_iota(jnp.int32, (width, width), 0)
+    row_lane = lax.broadcasted_iota(jnp.int32, (1, width), 1)
 
     def body(g, c):
-        hot = jnp.where(column == target_ref[g], 1.0, 0.0).astype(jnp.bfloat16)
+        at = row_lane
+        for j in range(group * bps):
+            t = g * group + j // bps
+            pos = meta_ref[t // per_peer, 0, per_peer + (t % per_peer) * bps + j % bps]
+            at = at + jnp.where(row_lane // cv == j, cv * (pos - j), 0)
+        hot = jnp.where(column == at, 1.0, 0.0).astype(jnp.bfloat16)
         if quant:
             code = part_ref[g].astype(jnp.int32)
             high = code >> 8
@@ -253,7 +424,8 @@
         if quant:
             factor = as_column(scale_ref[g], cv)
         for tl in range(group):
-            where = place_ref[req_ref[g * group + tl]]
+            t = g * group + tl
+            where = place_ref[meta_ref[t // per_peer, 0, t % per_peer]]
             rows = placed[tl * cv : (tl + 1) * cv]
             if quant:
                 rows = rows * factor
@@ -270,12 +442,12 @@
     lax.fori_loop(0, n, emit, 0)
 
 
-def gathered_rows(part, scale, target, requested, owners, n, send_max, group):
+def gathered_rows(part, scale, meta, owners, n, send_max, group, bps, per_peer):
     groups, cv, width = part.shape
     quant = scale is not None
-    args = [requested, owners, target, part] + ([scale] if quant else [])
+    args = [meta, owners, part] + ([scale] if quant else [])
     return pl.pallas_call(
-        functools.partial(gather_rows_kernel, (cv, group, send_max, quant)),
+        functools.partial(gather_rows_kernel, (cv, bps, per_peer, group, send_max, quant)),
         out_shape=[
             jax.ShapeDtypeStruct((n, send_max * cv, width), jnp.int16),
             jax.ShapeDtypeStruct((n, 1, LANES), jnp.float32),
@@ -327,25 +499,19 @@
 
     meta = jnp.concatenate([request.reshape(n, per_peer), col_pos.reshape(n, per_peer * bps)], axis=1)
     meta = jnp.pad(meta, ((0, 0), (0, LANES - meta.shape[1])))[:, None, :]
-    (meta_in,) = exchange([meta], gx, gy, 1)
-    requested = meta_in[:, 0, :per_peer].reshape(-1)
-    pos_in = meta_in[:, 0, per_peer : per_peer * (1 + bps)].reshape(slots // group, group * bps)
-    target = (cv * pos_in[:, :, None] + jnp.arange(cv, dtype=jnp.int32)).reshape(
-        slots // group, 1, group * bps * cv
-    )
-    answer = prolong[requested].reshape(n, per_peer * cv, dof)
-    (fetched,) = exchange([answer], gx, gy, 2)
-    fetched = fetched.reshape(slots, cv, dof)
-    made = products(fetched, stiffness, col_slot, group, quant)
     if quant:
-        part, scale = exchange(made, gx, gy, 3)
+        meta_in, part, scale = fused(meta, prolong, stiffness, col_slot, gx, gy, group)
     else:
-        flat = made[0].reshape(slots // group, cv, group, bps * cv).transpose(0, 2, 1, 3)
+        (meta_in,) = exchange([meta], gx, gy, 1)
+        answer = prolong[meta_in[:, 0, :per_peer].reshape(-1)].reshape(n, per_peer * cv, dof)
+        (fetched,) = exchange([answer], gx, gy, 2)
+        made = products(fetched.reshape(slots, cv, dof), stiffness, col_slot, group)
+        flat = made.reshape(slots // group, cv, group, bps * cv).transpose(0, 2, 1, 3)
         (flat,) = exchange([flat.reshape(n, per_peer * cv, bps * cv)], gx, gy, 3)
         flat = flat.reshape(slots // group, group, cv, bps * cv).transpose(0, 2, 1, 3)
         part, scale = flat.reshape(slots // group, cv, group * bps * cv), None
     code, factor = gathered_rows(
-        part, scale, target, requested, coarse_owner[:, 0], n, send_max, group
+        part, scale, meta_in, coarse_owner[:, 0], n, send_max, group, bps, per_peer
     )
     code, factor = exchange([code, factor], gx, gy, 4)
     return decoded(code, factor, cv)

time: 172 us -> 150 us (0.87)
  Pallas kernels: 158 us -> 142 us
  local copies, waits for them, and re-layouts: 12.5 us -> 8.21 us
    pallas_call x4 -> x1, Pallas kernels: 115 us -> 63.9 us  [exchange(): pl.pallas_call(functools.partial(exchange_kernel, gx, gy, count), out_sha...]
    pallas_call x2, Pallas kernels: 36.7 us -> 71.3 us  [the longest x1 53.1 us: fused(): pl.pallas_call(functools.partial(fused_kernel, (gx, gy, cv, bps, group)),...]
    unnamed x20 -> x14, local copies, waits for them, and re-layouts: 7.9 us -> 6.07 us
where the time goes in v2:
time: 150 us
  Pallas kernels  142 us (95%)
  local copies, waits for them, and re-layouts  8.21 us (5%)
    pallas_call x1, Pallas kernels, exchange(): pl.pallas_call(functools.partial(exchange_kernel, gx, gy, count), out_sha...  63.9 us
    pallas_call x1, Pallas kernels, fused(): pl.pallas_call(functools.partial(fused_kernel, (gx, gy, cv, bps, group)),...  53.1 us
    pallas_call x1, Pallas kernels, gathered_rows(): pl.pallas_call(functools.partial(gather_rows_kernel, (cv, bps, per_peer,...  18.2 us
    pallas_call x1, Pallas kernels, decoded(): pl.pallas_call(functools.partial(decode_kernel, cv), grid=(n // per_step,...  6.5 us
    unnamed x14, local copies, waits for them, and re-layouts  6.07 us

profile of v2, /device:TPU:15, one launch (start us, length us, event | category | flops | bytes accessed | tf_op | source)
XLA Modules:
  0.0 150.0 jit_solution(767013934540463080)
XLA Ops:
  0.0 0.7 reshape.10
  0.8 0.8 copy.8
  1.5 0.7 reshape.9.slot_ref
  2.2 0.8 copy.9
  3.0 0.1 reshape.11
  3.1 0.1 pad_add_fusion
  3.2 0.6 pad.4
  3.8 0.0 copy-start.5
  3.8 53.1 %fused.1 = (s32[32,1,128]{2,1,0:T(1,128)}, s16[32,24,384]{2,1,0:T(8,128)(2,1)}, f32[32,1,128]{2,1,0:T(1,128)}) custom-call(s32[512]{0:T(512)} %reshape.9.slot_ref, s32[32,1,128]{2,1,0:T(1,128)} %bitcast.3, bf16[64,24,128]{2,1,0:T(8,128)(2,1)} %prolong_ref.1, bf16[128,4,128,128]{3,2,1,0:T(8,128)(2,1)} %stiff_ref.1), custom_call_target="tpu_custom_call" | custom-call | tf_op jit(solution)/shard_map/fused/pallas_call | solution.py:336
  56.9 0.0 copy-done.5
  56.9 0.0 copy-start.1
  56.9 1.1 copy-done.1
  58.0 0.0 copy-start.3
  58.0 0.7 copy-done.3
  58.7 0.0 copy-start.4
  58.7 0.7 copy-done.4
  59.4 18.2 %gathered_rows.1 = (s16[32,96,384]{2,1,0:T(8,128)(2,1)S(1)}, f32[32,1,128]{2,1,0:T(1,128)S(1)}) custom-call(s32[32,1,128]{2,1,0:T(1,128)S(1)} %copy-done.3, s32[64]{0:T(128)S(1)} %bitcast.2, s16[32,24,384]{2,1,0:T(8,128)(2,1)S(1)} %copy-done.1, f32[32,1,128]{2,1,0:T(1,128)S(1)} %copy-done.4), custom_call_target="tpu_custom_call" | custom-call | tf_op jit(solution)/shard_map/gathered_rows/pallas_call | solution.py:449
  77.6 0.0 copy-start
  77.6 1.4 copy-done
  79.0 0.0 copy-start.2
  79.0 0.6 copy-done.2
  79.6 63.9 %exchange4.1 = (s16[32,96,384]{2,1,0:T(8,128)(2,1)}, f32[32,1,128]{2,1,0:T(1,128)}) custom-call(s16[32,96,384]{2,1,0:T(8,128)(2,1)} %copy-done, f32[32,1,128]{2,1,0:T(1,128)} %copy-done.2), custom_call_target="tpu_custom_call" | custom-call | tf_op jit(solution)/shard_map/exchange4/pallas_call | solution.py:73
  143.5 6.5 %decoded.1 = f32[128,24,384]{2,1,0:T(8,128)} custom-call(s16[32,96,384]{2,1,0:T(8,128)(2,1)} %get-tuple-element.17.code_ref, f32[32,1,128]{2,1,0:T(1,128)} %get-tuple-element.18.scale_ref), custom_call_target="tpu_custom_call" | custom-call | tf_op jit(solution)/shard_map/decoded/pallas_call | solution.py:478
Async XLA Ops:
  3.8 53.1 %copy-start.5 = (s32[64,1]{0,1:T(1,128)S(1)}, s32[64,1]{0,1:T(1,128)}, u32[]{:S(2)}) copy-start(s32[64,1]{0,1:T(1,128)} %param.11) | copy-start | bytes 772
  56.9 1.1 copy-start.1
  58.0 0.7 copy-start.3
  58.7 0.7 copy-start.4
  77.6 1.4 copy-start
  79.0 0.6 copy-start.2

commit v3 on v2

--- a/solution.py
+++ b/solution.py
@@ -16,6 +16,112 @@
 VMEM = pl.BlockSpec(memory_space=pltpu.VMEM)
 SMEM = pl.BlockSpec(memory_space=pltpu.SMEM)
 NT = (((1,), (1,)), ((), ()))
+
+
+def peer_at(k, gx, gy, mixed):
+    n = gx * gy
+    x, y = lax.axis_index("gx"), lax.axis_index("gy")
+    if gx % 2:
+        return lax.rem(x * gy + y + 1 + k, n)
+    half = gx // 2
+    count = half * gy
+    if mixed:
+        near, i = lax.rem(k, 2), k // 2
+    else:
+        near, i = k // count, lax.rem(k, count)
+    i = lax.rem(i + near, count)
+    side = lax.rem(x // half + 1 + near, 2)
+    row = side * half + lax.rem(x + i // gy, half)
+    return row * gy + lax.rem(y + i, gy)
+
+
+def deliver_kernel(dims, code_ref, scale_ref, out_ref, land_ref, land_scale, wide_ref, *sems):
+    gx, gy, cv = dims
+    code_send, code_recv, scale_send, scale_recv, out_sem = sems
+    n, rows, width = code_ref.shape
+    take = rows // cv
+    me = lax.axis_index("gx") * gy + lax.axis_index("gy")
+    barrier = pltpu.get_barrier_semaphore()
+
+    def where(peer):
+        return (peer // gy, lax.rem(peer, gy))
+
+    def greet(k, c):
+        peer = peer_at(k, gx, gy, True)
+        pl.semaphore_signal(barrier, inc=1, device_id=where(peer), device_id_type=MESH)
+        return c
+
+    lax.fori_loop(0, n - 1, greet, 0)
+
+    def copies(peer, source):
+        return [
+            pltpu.make_async_remote_copy(
+                src_ref=src.at[peer], dst_ref=dst.at[source],
+                send_sem=send.at[peer], recv_sem=recv.at[source],
+                device_id=where(peer), device_id_type=MESH,
+            )
+            for src, dst, send, recv in (
+                (scale_ref, land_scale, scale_send, scale_recv),
+                (code_ref, land_ref, code_send, code_recv),
+            )
+        ]
+
+    def out_copy(p):
+        at = pl.ds(p * take, take)
+        return pltpu.make_async_copy(wide_ref.at[at], out_ref.at[at], out_sem.at[p])
+
+    pl.semaphore_wait(barrier, n - 1)
+
+    def send(k, c):
+        for copy in copies(peer_at(k, gx, gy, True), me):
+            copy.start()
+        return c
+
+    lax.fori_loop(0, n - 1, send, 0)
+
+    def decode(code, scale, p):
+        values = code.astype(jnp.int32).astype(jnp.float32) * as_column(scale, rows)
+        wide_ref[pl.ds(p * take, take)] = values.reshape(take, cv, width)
+        out_copy(p).start()
+
+    decode(code_ref[me], scale_ref[me], me)
+
+    def drain(k, c):
+        source = peer_at(k, gx, gy, True)
+        for copy in copies(source, source):
+            copy.wait()
+        decode(land_ref[source], land_scale[source], source)
+        return c
+
+    lax.fori_loop(0, n - 1, drain, 0)
+
+    def finish(p, c):
+        out_copy(p).wait()
+        return c
+
+    lax.fori_loop(0, n, finish, 0)
+
+
+def delivered(code, scale, cv, gx, gy):
+    n, rows, width = code.shape
+    sem = pltpu.SemaphoreType.DMA
+    out = (n * rows // cv, cv, width)
+    return pl.pallas_call(
+        functools.partial(deliver_kernel, (gx, gy, cv)),
+        out_shape=jax.ShapeDtypeStruct(out, jnp.float32),
+        in_specs=[VMEM, VMEM],
+        out_specs=HBM,
+        scratch_shapes=[
+            pltpu.VMEM(code.shape, jnp.int16),
+            pltpu.VMEM(scale.shape, jnp.float32),
+            pltpu.VMEM(out, jnp.float32),
+        ]
+        + [sem((n,))] * 5,
+        compiler_params=pltpu.CompilerParams(
+            collective_id=4, has_side_effects=True, vmem_limit_bytes=40 << 20
+        ),
+        name="delivered",
+    )(code, scale)
 
 
 def exchange_kernel(gx, gy, count, *refs):
@@ -213,20 +319,24 @@
             device_id=where(peer), device_id_type=MESH,
         )
 
-    def meta_copy(k, peer, source):
-        return remote(meta_ref.at[peer], meta_out.at[source], meta_send.at[k], meta_recv.at[k], peer)
-
-    def fetch_copy(k, peer, source):
+    def meta_copy(peer, source):
+        return remote(
+            meta_ref.at[peer], meta_out.at[source], meta_send.at[peer], meta_recv.at[source], peer
+        )
+
+    def fetch_copy(peer, source):
         return remote(
             stage_ref.at[pl.ds(peer * group, group)],
             fetched_ref.at[pl.ds(source * group, group)],
-            fetch_send.at[k], fetch_recv.at[k], peer,
+            fetch_send.at[peer], fetch_recv.at[source], peer,
         )
 
-    def part_copies(k, peer, source):
+    def part_copies(peer, source):
         return (
-            remote(code_ref.at[peer], part_out.at[source], part_send.at[k], part_recv.at[k], peer),
-            remote(factor_ref.at[peer], scale_out.at[source], scale_send.at[k], scale_recv.at[k], peer),
+            remote(code_ref.at[peer], part_out.at[source], part_send.at[peer], part_recv.at[source], peer),
+            remote(
+                factor_ref.at[peer], scale_out.at[source], scale_send.at[peer], scale_recv.at[source], peer
+            ),
         )
 
     def mats_copy(peer):
@@ -245,70 +355,78 @@
     own_meta.start()
 
     def load(k, c):
-        mats_copy(lax.rem(me + k, n)).start()
-        return c
-
-    lax.fori_loop(1, n + 1, load, 0)
+        mats_copy(peer_at(k, gx, gy, False)).start()
+        return c
+
+    lax.fori_loop(0, n, load, 0)
     pl.semaphore_wait(barrier, n - 1)
 
     def ask(k, c):
-        meta_copy(k, lax.rem(me + k, n), me).start()
-        return c
-
-    lax.fori_loop(1, n, ask, 0)
+        meta_copy(peer_at(k, gx, gy, True), me).start()
+        return c
+
+    lax.fori_loop(0, n - 1, ask, 0)
     own_meta.wait()
 
     def asked(k, c):
-        meta_copy(k, lax.rem(me + n - k, n), lax.rem(me + n - k, n)).wait()
-        return c
-
-    lax.fori_loop(1, n, asked, 0)
+        source = peer_at(k, gx, gy, True)
+        meta_copy(source, source).wait()
+        return c
+
+    lax.fori_loop(0, n - 1, asked, 0)
     to_scalars = pltpu.make_async_copy(meta_out, req_ref, own_sem.at[1])
     to_scalars.start()
     to_scalars.wait()
 
     def fill(k, c):
-        peer = lax.rem(me + k, n)
+        peer = peer_at(k, gx, gy, True)
         for j in range(group):
             stage_ref[peer * group + j] = prolong_ref[req_ref[peer, 0, j]]
         return c
 
-    lax.fori_loop(1, n + 1, fill, 0)
+    lax.fori_loop(0, n, fill, 0)
 
     def answer(k, c):
-        fetch_copy(k, lax.rem(me + k, n), me).start()
-        return c
-
-    lax.fori_loop(1, n, answer, 0)
+        fetch_copy(peer_at(k, gx, gy, True), me).start()
+        return c
+
+    lax.fori_loop(0, n - 1, answer, 0)
     for j in range(group):
         wide_ref[me * group + j] = stage_ref[me * group + j].astype(jnp.float32)
 
     def take(k, c):
-        source = lax.rem(me + n - k, n)
-        fetch_copy(k, source, source).wait()
+        source = peer_at(k, gx, gy, True)
+        fetch_copy(source, source).wait()
         for j in range(group):
             wide_ref[source * group + j] = fetched_ref[source * group + j].astype(jnp.float32)
         return c
 
-    lax.fori_loop(1, n, take, 0)
-
-    def work(k, c):
-        peer = lax.rem(me + k, n)
-        mats_copy(peer).wait()
-        out = group_product(
-            (cv, bps, group), peer, slot_ref, wide_ref, cols_ref,
-            lambda tl: mats_ref[peer * group + tl],
-        )
-        code_ref[peer], factor_ref[peer] = coded(out)
-
-        @pl.when(k > 1)
+    lax.fori_loop(0, n - 1, take, 0)
+    wide_step = 2 if n % 2 == 0 else 1
+
+    def work(i, c):
+        for u in range(wide_step):
+            mats_copy(peer_at(i * wide_step + u, gx, gy, False)).wait()
+        for u in range(wide_step):
+            peer = peer_at(i * wide_step + u, gx, gy, False)
+            out = group_product(
+                (cv, bps, group), peer, slot_ref, wide_ref, cols_ref.at[u],
+                lambda tl: mats_ref[peer * group + tl],
+            )
+            code_ref[peer], factor_ref[peer] = coded(out)
+
+        @pl.when(i > 0)
         def _():
-            for copy in part_copies(k - 1, lax.rem(me + k - 1, n), me):
-                copy.start()
-
-        return c
-
-    lax.fori_loop(1, n + 1, work, 0)
+            for u in range(wide_step):
+                for copy in part_copies(peer_at((i - 1) * wide_step + u, gx, gy, False), me):
+                    copy.start()
+
+        return c
+
+    lax.fori_loop(0, n // wide_step, work, 0)
+    for k in range(n - wide_step, n - 1):
+        for copy in part_copies(peer_at(k, gx, gy, False), me):
+            copy.start()
     own = (
         pltpu.make_async_copy(code_ref.at[me], part_out.at[me], own_sem.at[2]),
         pltpu.make_async_copy(factor_ref.at[me], scale_out.at[me], own_sem.at[3]),
@@ -317,12 +435,12 @@
         copy.start()
 
     def drain(k, c):
-        source = lax.rem(me + n - k, n)
-        for copy in part_copies(k, source, source):
+        source = peer_at(k, gx, gy, False)
+        for copy in part_copies(source, source):
             copy.wait()
         return c
 
-    lax.fori_loop(1, n, drain, 0)
+    lax.fori_loop(0, n - 1, drain, 0)
     for copy in own:
         copy.wait()
 
@@ -347,7 +465,7 @@
             pltpu.VMEM((slots, cv, dof), jnp.bfloat16),
             pltpu.VMEM((slots, cv, dof), jnp.bfloat16),
             pltpu.VMEM((slots, cv, dof), jnp.float32),
-            pltpu.VMEM((group, LANES, dof), jnp.float32),
+            pltpu.VMEM((2, group, LANES, dof), jnp.float32),
             pltpu.VMEM((slots, bps, dof, dof), jnp.bfloat16),
             pltpu.VMEM((n, cv, width), jnp.int16),
             pltpu.VMEM((n, 1, LANES), jnp.float32),
@@ -432,14 +550,14 @@
             total_ref[where] = total_ref[where] + rows
         return c
 
-    lax.fori_loop(0, groups, body, 0)
+    lax.fori_loop(0, groups, body, 0, unroll=2)
 
     def emit(p, c):
         rows = total_ref[pl.ds(p * send_max, send_max)].reshape(send_max * cv, width)
         out_ref[p], out_scale_ref[p] = coded(rows)
         return c
 
-    lax.fori_loop(0, n, emit, 0)
+    lax.fori_loop(0, n, emit, 0, unroll=2)
 
 
 def gathered_rows(part, scale, meta, owners, n, send_max, group, bps, per_peer):
@@ -464,30 +582,6 @@
     )(*args)
 
 
-def decode_kernel(cv, code_ref, scale_ref, out_ref):
-    per_step, rows, width = code_ref.shape
-
-    for p in range(per_step):
-        values = code_ref[p].astype(jnp.int32).astype(jnp.float32) * as_column(scale_ref[p], rows)
-        out_ref[p * (rows // cv) : (p + 1) * (rows // cv)] = values.reshape(rows // cv, cv, width)
-
-
-def decoded(code, scale, cv):
-    n, rows, width = code.shape
-    per_step = 4 if n % 4 == 0 else 1
-    return pl.pallas_call(
-        functools.partial(decode_kernel, cv),
-        grid=(n // per_step,),
-        out_shape=jax.ShapeDtypeStruct((n * rows // cv, cv, width), jnp.float32),
-        in_specs=[
-            pl.BlockSpec((per_step, rows, width), lambda i: (i, 0, 0)),
-            pl.BlockSpec((per_step, 1, LANES), lambda i: (i, 0, 0)),
-        ],
-        out_specs=pl.BlockSpec((per_step * rows // cv, cv, width), lambda i: (i, 0, 0)),
-        name="decoded",
-    )(code, scale)
-
-
 def per_device(gx, gy, prolong, stiffness, request, col_slot, col_pos, coarse_owner):
     n = gx * gy
     own_aggs, cv, dof = prolong.shape
@@ -513,8 +607,7 @@
     code, factor = gathered_rows(
         part, scale, meta_in, coarse_owner[:, 0], n, send_max, group, bps, per_peer
     )
-    code, factor = exchange([code, factor], gx, gy, 4)
-    return decoded(code, factor, cv)
+    return delivered(code, factor, cv, gx, gy)
 
 
 def solution(mesh):

time: 150 us -> 140 us (0.933)
  Pallas kernels: 142 us -> 130 us
    pallas_call x2 -> x1, Pallas kernels: 70.4 us -> 64.3 us  [delivered(): pl.pallas_call(functools.partial(deliver_kernel, (gx, gy, cv)), out_shape...]
    pallas_call x1, Pallas kernels: 18.2 us -> 13.8 us  [gathered_rows(): pl.pallas_call(functools.partial(gather_rows_kernel, (cv, bps, per_peer,...]
    unnamed x14 -> x11, local copies, waits for them, and re-layouts: 6.07 us -> 6.26 us
where the time goes in v3:
time: 140 us; the launch traced here: 139 us
  Pallas kernels  130 us (93%)
  local copies, waits for them, and re-layouts  8.39 us (6%)
    pallas_call x1, Pallas kernels, delivered(): pl.pallas_call(functools.partial(deliver_kernel, (gx, gy, cv)), out_shape...  64.3 us
    pallas_call x1, Pallas kernels, fused(): pl.pallas_call(functools.partial(fused_kernel, (gx, gy, cv, bps, group)),...  52.1 us
    pallas_call x1, Pallas kernels, gathered_rows(): pl.pallas_call(functools.partial(gather_rows_kernel, (cv, bps, per_peer,...  13.8 us
    unnamed x11, local copies, waits for them, and re-layouts  6.26 us

profile of v3, /device:TPU:15, one launch (start us, length us, event | category | flops | bytes accessed | tf_op | source)
XLA Modules:
  0.0 138.8 jit_solution(3987564497993749364)
XLA Ops:
  0.0 0.7 reshape.10
  0.8 0.8 copy.8
  1.5 0.7 reshape.9.slot_ref
  2.2 0.8 copy.9
  3.0 0.1 reshape.11
  3.1 0.1 pad_add_fusion
  3.2 0.6 pad.4
  3.8 0.0 copy-start.3
  3.8 52.1 %fused.1 = (s32[32,1,128]{2,1,0:T(1,128)}, s16[32,24,384]{2,1,0:T(8,128)(2,1)}, f32[32,1,128]{2,1,0:T(1,128)}) custom-call(s32[512]{0:T(512)} %reshape.9.slot_ref, s32[32,1,128]{2,1,0:T(1,128)} %bitcast.3, bf16[64,24,128]{2,1,0:T(8,128)(2,1)} %prolong_ref.1, bf16[128,4,128,128]{3,2,1,0:T(8,128)(2,1)} %stiff_ref.1), custom_call_target="tpu_custom_call" | custom-call | tf_op jit(solution)/shard_map/fused/pallas_call | solution.py:454
  55.9 0.0 copy-done.3
  55.9 0.0 copy-start
  55.9 1.1 copy-done
  57.0 0.0 copy-start.1
  57.0 0.7 copy-done.1
  57.7 0.0 copy-start.2
  57.7 0.7 copy-done.2
  58.4 13.8 %gathered_rows.1 = (s16[32,96,384]{2,1,0:T(8,128)(2,1)S(1)}, f32[32,1,128]{2,1,0:T(1,128)S(1)}) custom-call(s32[32,1,128]{2,1,0:T(1,128)S(1)} %copy-done.1, s32[64]{0:T(128)S(1)} %bitcast.2, s16[32,24,384]{2,1,0:T(8,128)(2,1)S(1)} %copy-done, f32[32,1,128]{2,1,0:T(1,128)S(1)} %copy-done.2), custom_call_target="tpu_custom_call" | custom-call | tf_op jit(solution)/shard_map/gathered_rows/pallas_call | solution.py:567
  72.3 64.3 %delivered.1 = f32[128,24,384]{2,1,0:T(8,128)S(1)} custom-call(s16[32,96,384]{2,1,0:T(8,128)(2,1)S(1)} %get-tuple-element.13.code_ref, f32[32,1,128]{2,1,0:T(1,128)S(1)} %get-tuple-element.14.scale_ref), custom_call_target="tpu_custom_call" | custom-call | tf_op jit(solution)/shard_map/delivered/pallas_call | solution.py:109
  136.6 2.2 %copy.11 = f32[128,24,384]{2,1,0:T(8,128)} copy(f32[128,24,384]{2,1,0:T(8,128)S(1)} %delivered.1) | data formatting | bytes 9437184
Async XLA Ops:
  3.8 52.1 %copy-start.3 = (s32[64,1]{0,1:T(1,128)S(1)}, s32[64,1]{0,1:T(1,128)}, u32[]{:S(2)}) copy-start(s32[64,1]{0,1:T(1,128)} %param.11) | copy-start | bytes 772
  55.9 1.1 copy-start
  57.0 0.7 copy-start.1
  57.7 0.7 copy-start.2

commit v4 on v3

--- a/solution.py
+++ b/solution.py
@@ -218,7 +218,7 @@
     applied = []
     for tl in range(group):
         for q in range(bps):
-            block = wide_ref[slot_ref[(grp * group + tl) * bps + q]]
+            block = wide_ref[slot_ref[grp * group + tl, q]]
             at = (span * tl + cv * q) % LANES
             first = min(cv, LANES - at)
             cols_ref[tl, at : at + first, :] = block[:first]
@@ -294,7 +294,7 @@
         ],
         compiler_params=pltpu.CompilerParams(vmem_limit_bytes=48 << 20),
         name="products",
-    )(col_slot.reshape(-1), fetched, stiffness)
+    )(col_slot, fetched, stiffness)
 
 
 def fused_kernel(
@@ -476,7 +476,7 @@
             collective_id=1, has_side_effects=True, vmem_limit_bytes=56 << 20
         ),
         name="fused",
-    )(col_slot.reshape(-1), meta, prolong, stiffness)
+    )(col_slot, meta, prolong, stiffness)
 
 
 def gather_rows_kernel(dims, meta_ref, owner_ref, part_ref, *refs):
@@ -550,14 +550,14 @@
             total_ref[where] = total_ref[where] + rows
         return c
 
-    lax.fori_loop(0, groups, body, 0, unroll=2)
+    lax.fori_loop(0, groups, body, 0, unroll=4)
 
     def emit(p, c):
         rows = total_ref[pl.ds(p * send_max, send_max)].reshape(send_max * cv, width)
         out_ref[p], out_scale_ref[p] = coded(rows)
         return c
 
-    lax.fori_loop(0, n, emit, 0, unroll=2)
+    lax.fori_loop(0, n, emit, 0, unroll=4)
 
 
 def gathered_rows(part, scale, meta, owners, n, send_max, group, bps, per_peer):

time: 140 us -> 138 us (0.986)
  Pallas kernels: 130 us -> 128 us
    pallas_call x1, Pallas kernels: 13.8 us -> 11.2 us  [gathered_rows(): pl.pallas_call(functools.partial(gather_rows_kernel, (cv, bps, per_peer,...]
where the time goes in v4:
time: 138 us; the launch traced here: 137 us
  Pallas kernels  128 us (93%)
  local copies, waits for them, and re-layouts  8.33 us (6%)
    pallas_call x1, Pallas kernels, delivered(): pl.pallas_call(functools.partial(deliver_kernel, (gx, gy, cv)), out_shape...  64.3 us
    pallas_call x1, Pallas kernels, fused(): pl.pallas_call(functools.partial(fused_kernel, (gx, gy, cv, bps, group)),...  53 us
    pallas_call x1, Pallas kernels, gathered_rows(): pl.pallas_call(functools.partial(gather_rows_kernel, (cv, bps, per_peer,...  11.2 us
    unnamed x11, local copies, waits for them, and re-layouts  6.89 us

profile of v4, /device:TPU:15, one launch (start us, length us, event | category | flops | bytes accessed | tf_op | source)
XLA Modules:
  0.0 136.9 jit_solution(18051525778887870192)
XLA Ops:
  0.0 0.7 reshape.6
  0.8 1.4 %copy.10.slot_ref = s32[128,4]{1,0:T(8,128)} copy(s32[128,4]{0,1:T(4,128)} %param.9) | data formatting | bytes 4096 | tf_op args[3]
  2.2 0.8 copy.9
  3.0 0.1 reshape.7
  3.0 0.1 pad_add_fusion
  3.1 0.6 pad.4
  3.7 0.0 copy-start.3
  3.7 53.0 %fused.1 = (s32[32,1,128]{2,1,0:T(1,128)}, s16[32,24,384]{2,1,0:T(8,128)(2,1)}, f32[32,1,128]{2,1,0:T(1,128)}) custom-call(s32[128,4]{1,0:T(8,128)} %copy.10.slot_ref, s32[32,1,128]{2,1,0:T(1,128)} %bitcast.3, bf16[64,24,128]{2,1,0:T(8,128)(2,1)} %prolong_ref.1, bf16[128,4,128,128]{3,2,1,0:T(8,128)(2,1)} %stiff_ref.1), custom_call_target="tpu_custom_call" | custom-call | tf_op jit(solution)/shard_map/fused/pallas_call | solution.py:454
  56.7 0.0 copy-done.3
  56.7 0.0 copy-start
  56.7 1.1 copy-done
  57.8 0.0 copy-start.1
  57.8 0.7 copy-done.1
  58.5 0.0 copy-start.2
  58.5 0.7 copy-done.2
  59.2 11.2 %gathered_rows.1 = (s16[32,96,384]{2,1,0:T(8,128)(2,1)S(1)}, f32[32,1,128]{2,1,0:T(1,128)S(1)}) custom-call(s32[32,1,128]{2,1,0:T(1,128)S(1)} %copy-done.1, s32[64]{0:T(128)S(1)} %bitcast.2, s16[32,24,384]{2,1,0:T(8,128)(2,1)S(1)} %copy-done, f32[32,1,128]{2,1,0:T(1,128)S(1)} %copy-done.2), custom_call_target="tpu_custom_call" | custom-call | tf_op jit(solution)/shard_map/gathered_rows/pallas_call | solution.py:567
  70.5 64.3 %delivered.1 = f32[128,24,384]{2,1,0:T(8,128)S(1)} custom-call(s16[32,96,384]{2,1,0:T(8,128)(2,1)S(1)} %get-tuple-element.13.code_ref, f32[32,1,128]{2,1,0:T(1,128)S(1)} %get-tuple-element.14.scale_ref), custom_call_target="tpu_custom_call" | custom-call | tf_op jit(solution)/shard_map/delivered/pallas_call | solution.py:109
  134.7 2.2 %copy.12 = f32[128,24,384]{2,1,0:T(8,128)} copy(f32[128,24,384]{2,1,0:T(8,128)S(1)} %delivered.1) | data formatting | bytes 9437184
Async XLA Ops:
  3.7 53.0 %copy-start.3 = (s32[64,1]{0,1:T(1,128)S(1)}, s32[64,1]{0,1:T(1,128)}, u32[]{:S(2)}) copy-start(s32[64,1]{0,1:T(1,128)} %param.11) | copy-start | bytes 772
  56.7 1.1 copy-start
  57.8 0.7 copy-start.1
  58.5 0.7 copy-start.2
